TPU v7x, 32 devices: a whole 2x2x4 slice. The times are simulated.
32 devices in a mesh: wide: 8 (over z, x), narrow: 4 (over y, core).
Axes of the slice: x: 2, y: 2, z: 4, core: 2. Of those that a mesh axis runs over, the one named last changes fastest.
Arguments:
- positions: float32 [3, 4096], P(None, ('wide', 'narrow')), may hold values from -1 to 69, as said below
- noise: float32 [3, 16, 4096], P(None, None, ('wide', 'narrow')), may hold values from -6 to 6
Outputs:
- displacement: float32 [3, 16, 4096], P(None, None, ('wide', 'narrow'))
Inputs may be any that keep to these rules, and one draw needn't show every extreme that they name: `positions`: any two particles lie at least 1.2 apart.
All inputs are finite; a program needn't handle non-finite values.
Results may differ from a plain program's by a relative error of at most 0.0003.
Values sent between devices are 32-bit elements; how exact they have to be, the bound alone decides.
A program may use at most 64 MiB of HBM per device.

v0:
```python
import math

import jax
import jax.numpy as jnp
from jax import lax
from jax.sharding import PartitionSpec as P

ITERS = 3
ROOT_STEPS = 30


highest = lax.Precision.HIGHEST


def tile_factors(dist_sq, itself):
    safe_sq = jnp.where(itself, 4.0, dist_sq)
    radial = jnp.sqrt(safe_sq)
    inverse = 1.0 / radial
    far_scalar = 0.75 * inverse + 0.5 * inverse * inverse * inverse
    far_outer = (0.75 * inverse - 1.5 * inverse * inverse * inverse) * inverse * inverse
    near_scalar = 1.0 - 0.28125 * radial
    near_outer = 0.09375 * inverse
    nearby = radial < 2.0
    scalar = jnp.where(itself, 1.0, jnp.where(nearby, near_scalar, far_scalar))
    outer_part = jnp.where(itself, 0.0, jnp.where(nearby, near_outer, far_outer))
    return (scalar, outer_part)


def contract(left, kernel):
    return lax.dot_general(
        left,
        kernel,
        (((1,), (1,)), ((), ())),
        precision=highest,
        preferred_element_type=jnp.float32,
    )


def tile_product(row_pos, row_ids, col_pos, col_ids, vectors):
    width = vectors.shape[1]
    delta = row_pos[:, :, None] - col_pos[:, None, :]
    dist_sq = delta[0] * delta[0] + delta[1] * delta[1] + delta[2] * delta[2]
    itself = row_ids[:, None] == col_ids[None, :]
    scalar, outer_part = tile_factors(dist_sq, itself)
    result = []
    for component in range(3):
        diag_kernel = scalar + outer_part * delta[component] * delta[component]
        result.append(contract(vectors[component], diag_kernel))
    for first, second in ((0, 1), (0, 2), (1, 2)):
        cross = outer_part * delta[first] * delta[second]
        both = contract(jnp.concatenate([vectors[second], vectors[first]], axis=0), cross)
        result[first] = result[first] + both[:width]
        result[second] = result[second] + both[width:]
    return jnp.stack(result)


def blocked_product(row_pos, row_ids, col_pos, col_ids, vectors):
    rows = row_pos.shape[1]
    block = math.gcd(rows, 512)

    def row_block(index):
        begin = index * block
        pos_block = lax.dynamic_slice_in_dim(row_pos, begin, block, 1)
        id_block = lax.dynamic_slice_in_dim(row_ids, begin, block, 0)
        return tile_product(pos_block, id_block, col_pos, col_ids, vectors)

    pieces = lax.map(row_block, jnp.arange(rows // block, dtype=jnp.int32))
    return jnp.moveaxis(pieces, 0, 2).reshape(3, vectors.shape[1], rows)


def gram_of(left, right):
    return jnp.einsum("asp,atp->st", left, right, precision=highest)


def stacked_gram(stacked, right):
    return jnp.einsum("kasp,atp->kst", stacked, right, precision=highest)


def stacked_remove(stacked, weights):
    return jnp.einsum("kasp,kst->atp", stacked, weights, precision=highest)


def block_remove(member, weights):
    return jnp.einsum("asp,st->atp", member, weights, precision=highest)


def rotate(block, matrix):
    return jnp.einsum("atp,ts->asp", block, matrix, precision=highest)


def cholesky_pair(gram):
    order = gram.shape[0]
    places = jnp.arange(order, dtype=jnp.int32)
    lower = jnp.zeros((order, order), jnp.float32)
    for column in range(order):
        needed = gram[:, column] - jnp.dot(
            lower, lower[column, :], precision=highest, preferred_element_type=jnp.float32
        )
        pivot = jnp.sqrt(needed[column])
        entries = jnp.where(places >= column, needed / pivot, 0.0)
        marker = (places == column).astype(jnp.float32)
        lower = lower + entries[:, None] * marker[None, :]
    solved = jnp.zeros((order, order), jnp.float32)
    for row in range(order):
        marker = (places == row).astype(jnp.float32)
        fresh = (
            marker
            - jnp.dot(lower[row, :], solved, precision=highest, preferred_element_type=jnp.float32)
        ) / lower[row, row]
        solved = solved + marker[:, None] * fresh[None, :]
    return (lower.T, solved.T)


def tridiagonal(diagonal_blocks, lower_blocks):
    width = diagonal_blocks[0].shape[0]
    order = len(diagonal_blocks) * width
    matrix = jnp.zeros((order, order), jnp.float32)
    for index, block in enumerate(diagonal_blocks):
        offset = index * width
        matrix = matrix.at[offset : offset + width, offset : offset + width].set(block)
    for index, block in enumerate(lower_blocks):
        offset = index * width
        matrix = matrix.at[offset + width : offset + 2 * width, offset : offset + width].set(block)
        matrix = matrix.at[offset : offset + width, offset + width : offset + 2 * width].set(
            block.T
        )
    return matrix


def matrix_root(matrix):
    identity = jnp.eye(matrix.shape[0], dtype=jnp.float32)
    scale = jnp.sqrt(jnp.sum(matrix * matrix))

    def newton(turn, carry):
        current, other = carry
        factor = 1.5 * identity - 0.5 * jnp.dot(
            other, current, precision=highest, preferred_element_type=jnp.float32
        )
        return (
            jnp.dot(current, factor, precision=highest, preferred_element_type=jnp.float32),
            jnp.dot(factor, other, precision=highest, preferred_element_type=jnp.float32),
        )

    current, other = lax.fori_loop(0, ROOT_STEPS, newton, (matrix / scale, identity))
    return current * jnp.sqrt(scale)


def first_pass(basis, image):
    work = image
    single = None
    for member in basis:
        single = lax.psum(gram_of(member, work), ("wide", "narrow"))
        work = work - block_remove(member, single)
    return (single, work)


def second_pass(basis, work):
    stacked = jnp.stack(basis)
    again, raw_gram = lax.psum(
        (stacked_gram(stacked, work), gram_of(work, work)), ("wide", "narrow")
    )
    work = work - stacked_remove(stacked, again)
    gram = raw_gram - jnp.einsum("kst,ksu->tu", again, again, precision=highest)
    return (work, gram)


def per_device(positions, noise):
    width = noise.shape[1]
    local = noise.shape[2]
    narrow_count = lax.axis_size("narrow")
    row_pos = lax.all_gather(positions, "narrow", axis=1, tiled=True)
    col_pos = lax.all_gather(positions, "wide", axis=1, tiled=True)
    row_ids = lax.axis_index("wide") * (narrow_count * local) + jnp.arange(
        narrow_count * local, dtype=jnp.int32
    )
    places = jnp.arange(col_pos.shape[1], dtype=jnp.int32)
    col_ids = (
        places // local * (narrow_count * local) + lax.axis_index("narrow") * local + places % local
    )
    noise_gram = lax.psum(gram_of(noise, noise), ("wide", "narrow"))
    start_upper, start_inverse = cholesky_pair(noise_gram)
    basis = [rotate(noise, start_inverse)]
    diagonal_blocks = []
    lower_blocks = []
    for index in range(ITERS):
        empty = jnp.zeros((3, width, row_pos.shape[1]), jnp.float32)
        partial_rows = empty + blocked_product(
            row_pos,
            row_ids,
            col_pos,
            col_ids,
            lax.all_gather(basis[index], "wide", axis=2, tiled=True),
        )
        product = lax.psum_scatter(partial_rows, "narrow", scatter_dimension=2, tiled=True)
        if index + 1 == ITERS:
            current_block = lax.psum(gram_of(basis[index], product), ("wide", "narrow"))
            diagonal_blocks.append(0.5 * (current_block + current_block.T))
        else:
            current_block, work = first_pass(basis, product)
            diagonal_blocks.append(0.5 * (current_block + current_block.T))
            work, gram = second_pass(basis, work)
            upper, inverse = cholesky_pair(gram)
            lower_blocks.append(upper)
            basis.append(rotate(work, inverse))
    root = matrix_root(tridiagonal(diagonal_blocks, lower_blocks))
    mixing = jnp.dot(
        root[:, :width], start_upper, precision=highest, preferred_element_type=jnp.float32
    ).reshape(ITERS, width, width)
    return jnp.einsum("katp,kts->asp", jnp.stack(basis), mixing, precision=highest)


def solution(mesh):
    return jax.shard_map(
        per_device,
        mesh=mesh,
        in_specs=(P(None, ("wide", "narrow")), P(None, None, ("wide", "narrow"))),
        out_specs=P(None, None, ("wide", "narrow")),
        check_vma=False,
    )
```

profile of v0, /device:TPU:0, one launch (start us, length us, event | category | flops | bytes accessed | tf_op | source)
XLA Modules:
  0.0 678.2 jit_solution(14943982212568380633)
XLA Ops:
  6.5 28.2 %all_gather.17 = f32[3,1024]{1,0:T(4,128)S(1)} all-gather(f32[3,128]{1,0:T(4,128)} %param.18), channel_id=1, replica_groups=mesh['wide'=8,'narrow'=4] {'wide'}, dimensions={1}, use_global_device_ids=true | all-gather | bytes 13824 | tf_op jit(solution)/shard_map/all_gather | solution.py:172
  34.7 5.3 all_gather.16
  40.5 4.1 fusion.9
  44.6 3.1 bitcast_multiply_fusion.4
  47.8 2.9 bitcast_multiply_fusion.1
  50.9 38.9 %psum.63 = f32[16,16]{1,0:T(8,128)S(1)} all-reduce(f32[16,16]{1,0:T(8,128)S(1)} %convolution_bitcast_fusion.16), channel_id=1, replica_groups=mesh['wide'=8,'narrow'=4] {'wide','narrow'}, use_global_device_ids=true, to_apply=%region_0.1 | all-reduce | flops 256 | bytes 2048 | tf_op jit(solution)/shard_map/psum | solution.py:180
  119.2 0.9 fusion.142
  122.6 1.0 fusion.146
  125.3 0.9 fusion.149
  128.0 30.8 %all_gather.15 = f32[3,16,1024]{2,1,0:T(8,128)S(1)} all-gather(f32[3,16,128]{2,1,0:T(8,128)S(1)} %bitcast.1264), channel_id=1, replica_groups=mesh['wide'=8,'narrow'=4] {'wide'}, dimensions={2}, use_global_device_ids=true | all-gather | bytes 221184 | tf_op jit(solution)/shard_map/all_gather | solution.py:192
  158.8 3.7 fusion.190
  162.6 2.0 fusion.192
  164.6 2.0 fusion.191
  166.6 3.2 fusion.13
  169.9 1.8 fusion.24
  171.7 1.9 fusion.22
  173.6 1.8 fusion.20
  177.5 17.6 %reduce-scatter.4.cloned.1.call-done = f32[3,16,128]{2,1,0:T(8,128)} async-done(((f32[3,16,512]{2,1,0:T(8,128)}), f32[3,16,128]{2,1,0:T(8,128)}) %reduce-scatter.4.cloned.1.call-update) | async-done | bytes 24592 | tf_op jit(solution)/shard_map/reduce_scatter | solution.py:194
  196.0 39.4 %psum.64 = f32[16,16]{1,0:T(8,128)S(1)} all-reduce(f32[16,16]{1,0:T(8,128)S(1)} %convolution_bitcast_fusion.15), channel_id=1, replica_groups=mesh['wide'=8,'narrow'=4] {'wide','narrow'}, use_global_device_ids=true, to_apply=%region_2.3 | all-reduce | flops 256 | bytes 2048 | tf_op jit(solution)/shard_map/psum | solution.py:152
  235.3 1.0 fusion.41
  236.6 41.5 %all-reduce.2 = (f32[16,16]{1,0:T(8,128)S(1)}, f32[16,16]{1,0:T(8,128)S(1)}) all-reduce(f32[16,16]{1,0:T(8,128)S(1)} %convolution_bitcast_fusion.13, f32[16,16]{1,0:T(8,128)S(1)} %convolution_bitcast_fusion.14), channel_id=1, replica_groups=mesh['wide'=8,'narrow'=4] {'wide','narrow'}, use_global_device_ids=true, to_apply=%region_4.5 | all-reduce | flops 512 | bytes 4096 | tf_op jit(solution)/shard_map/psum | solution.py:159
  307.1 0.9 fusion.157
  316.6 30.6 %all_gather.18 = f32[3,16,1024]{2,1,0:T(8,128)S(1)} all-gather(f32[3,16,128]{2,1,0:T(8,128)S(1)} %bitcast.1268), channel_id=1, replica_groups=mesh['wide'=8,'narrow'=4] {'wide'}, dimensions={2}, use_global_device_ids=true | all-gather | bytes 221184 | tf_op jit(solution)/shard_map/all_gather | solution.py:192
  347.3 2.0 fusion.187
  349.3 2.0 fusion.189
  351.4 2.0 fusion.188
  353.4 1.8 fusion.30
  355.3 1.8 fusion.28
  357.1 1.9 fusion.26
  359.9 19.5 %reduce-scatter.6.cloned.1.call-done = f32[3,16,128]{2,1,0:T(8,128)} async-done(((f32[3,16,512]{2,1,0:T(8,128)}), f32[3,16,128]{2,1,0:T(8,128)}) %reduce-scatter.6.cloned.1.call-update) | async-done | bytes 24592 | tf_op jit(solution)/shard_map/reduce_scatter | solution.py:194
  380.3 39.4 %psum.67 = f32[16,16]{0,1:T(8,128)S(1)} all-reduce(f32[16,16]{0,1:T(8,128)S(1)} %convolution_bitcast_fusion.12), channel_id=1, replica_groups=mesh['wide'=8,'narrow'=4] {'wide','narrow'}, use_global_device_ids=true, to_apply=%region_6.7 | all-reduce | flops 256 | bytes 2048 | tf_op jit(solution)/shard_map/psum | solution.py:152
  419.6 0.9 fusion.39
  420.7 41.1 %psum.68 = f32[16,16]{0,1:T(8,128)S(1)} all-reduce(f32[16,16]{0,1:T(8,128)S(1)} %convolution_bitcast_fusion.11), channel_id=1, replica_groups=mesh['wide'=8,'narrow'=4] {'wide','narrow'}, use_global_device_ids=true, to_apply=%region_7.8 | all-reduce | flops 256 | bytes 2048 | tf_op jit(solution)/shard_map/psum | solution.py:152
  462.3 39.5 %all-reduce.1 = (f32[2,16,16]{2,1,0:T(8,128)S(1)}, f32[16,16]{1,0:T(8,128)S(1)}) all-reduce(f32[2,16,16]{2,1,0:T(8,128)S(1)} %convolution_bitcast_fusion.7, f32[16,16]{1,0:T(8,128)S(1)} %convolution_bitcast_fusion.10), channel_id=1, replica_groups=mesh['wide'=8,'narrow'=4] {'wide','narrow'}, use_global_device_ids=true, to_apply=%region_9.10 | all-reduce | flops 768 | bytes 6144 | tf_op jit(solution)/shard_map/psum | solution.py:159
  530.7 0.9 fusion.173
  540.3 30.8 %all_gather.19 = f32[3,16,1024]{2,1,0:T(8,128)S(1)} all-gather(f32[3,16,128]{2,1,0:T(8,128)S(1)} %bitcast.1272), channel_id=1, replica_groups=mesh['wide'=8,'narrow'=4] {'wide'}, dimensions={2}, use_global_device_ids=true | all-gather | bytes 221184 | tf_op jit(solution)/shard_map/all_gather | solution.py:192
  571.1 2.0 fusion.184
  573.1 2.0 fusion.186
  575.2 2.0 fusion.185
  577.2 1.8 fusion.36
  579.0 1.8 fusion.34
  580.9 1.9 fusion.32
  584.3 19.2 %reduce-scatter.8.cloned.1.call-done = f32[3,16,128]{2,1,0:T(8,128)} async-done(((f32[3,16,512]{2,1,0:T(8,128)}), f32[3,16,128]{2,1,0:T(8,128)}) %reduce-scatter.8.cloned.1.call-update) | async-done | bytes 24592 | tf_op jit(solution)/shard_map/reduce_scatter | solution.py:194
  604.4 39.6 %psum.71 = f32[16,16]{0,1:T(8,128)S(1)} all-reduce(f32[16,16]{0,1:T(8,128)S(1)} %convolution_bitcast_fusion.8), channel_id=1, replica_groups=mesh['wide'=8,'narrow'=4] {'wide','narrow'}, use_global_device_ids=true, to_apply=%region_11.12 | all-reduce | flops 256 | bytes 2048 | tf_op jit(solution)/shard_map/psum | solution.py:196
  645.4 1.9 dynamic-slice_select_fusion
  647.3 2.0 scatter.30
  652.4 17.9 %while.15 = (s32[]{:T(128)}, f32[48,48]{0,1:T(8,128)S(1)}, f32[48,48]{1,0:T(8,128)S(1)}, s32[]{:T(128)}) while((s32[]{:T(128)}, f32[48,48]{0,1:T(8,128)S(1)}, f32[48,48]{1,0:T(8,128)S(1)}, s32[]{:T(128)}) %tuple.168), condition=%wide.region_15.16_spmd.clone, body=%wide.region_14.15_spmd.clone.sunk | while | flops 3990530 | bytes 119861 | solution.py:144
  670.5 0.9 convolution_bitcast_fusion.1
  (491 shorter events, 107.3 us)
Async XLA Ops:
  6.5 44.2 %copy-start = (f32[3,16,128]{2,1,0:T(8,128)S(1)}, f32[3,16,128]{2,1,0:T(8,128)}, u32[]{:S(2)}) copy-start(f32[3,16,128]{2,1,0:T(8,128)} %param.19) | copy-start | bytes 73732
  6.5 188.5 %reduce-scatter.4.cloned.1.call-start = ((), (), s32[]{:S(2)}) async-start(), calls=%async_computation.3 | async-start | bytes 122880 | tf_op jit(solution)/shard_map/reduce_scatter | solution.py:194
  40.5 7.3 %copy-start.1 = (f32[3,512,1024]{2,1,0:T(8,128)}, f32[3,512,1024]{2,1,0:T(8,128)S(1)}, u32[]{:S(2)}) copy-start(f32[3,512,1024]{2,1,0:T(8,128)S(1)} %broadcast_subtract_fusion) | copy-start | bytes 18874372
  110.4 52.2 %copy-start.6 = (f32[512,1024]{1,0:T(8,128)S(1)}, f32[512,1024]{1,0:T(8,128)}, u32[]{:S(2)}) copy-start(f32[512,1024]{1,0:T(8,128)} %get-tuple-element.254) | copy-start | bytes 6291460
  122.6 42.0 %copy-start.3 = (f32[512,1024]{1,0:T(8,128)S(1)}, f32[512,1024]{1,0:T(8,128)}, u32[]{:S(2)}) copy-start(f32[512,1024]{1,0:T(8,128)} %get-tuple-element.250) | copy-start | bytes 6291460
  158.8 7.8 %copy-start.2 = (f32[3,512,1024]{2,1,0:T(8,128)S(1)}, f32[3,512,1024]{2,1,0:T(8,128)}, u32[]{:S(2)}) copy-start(f32[3,512,1024]{2,1,0:T(8,128)} %copy-done.1) | copy-start | bytes 18874372
  169.9 3.7 copy-start.11
  169.9 3.7 copy-start.14
  176.2 203.2 %reduce-scatter.6.cloned.1.call-start = ((), (), s32[]{:S(2)}) async-start(), calls=%async_computation.4 | async-start | bytes 122880 | tf_op jit(solution)/shard_map/reduce_scatter | solution.py:194
  280.8 66.5 %copy-start.9 = (f32[512,1024]{1,0:T(8,128)S(1)}, f32[512,1024]{1,0:T(8,128)}, u32[]{:S(2)}) copy-start(f32[512,1024]{1,0:T(8,128)} %get-tuple-element.255) | copy-start | bytes 6291460
  309.6 39.7 %copy-start.7 = (f32[512,1024]{1,0:T(8,128)S(1)}, f32[512,1024]{1,0:T(8,128)}, u32[]{:S(2)}) copy-start(f32[512,1024]{1,0:T(8,128)} %get-tuple-element.254) | copy-start | bytes 6291460
  347.3 4.1 copy-start.4
  349.3 4.1 copy-start.15
  351.4 3.9 copy-start.12
  359.7 243.9 %reduce-scatter.8.cloned.1.call-start = ((), (), s32[]{:S(2)}) async-start(), calls=%async_computation.5 | async-start | bytes 122880 | tf_op jit(solution)/shard_map/reduce_scatter | solution.py:194
  504.4 66.6 %copy-start.10 = (f32[512,1024]{1,0:T(8,128)S(1)}, f32[512,1024]{1,0:T(8,128)}, u32[]{:S(2)}) copy-start(f32[512,1024]{1,0:T(8,128)} %get-tuple-element.255) | copy-start | bytes 6291460
  533.2 39.9 %copy-start.8 = (f32[512,1024]{1,0:T(8,128)S(1)}, f32[512,1024]{1,0:T(8,128)}, u32[]{:S(2)}) copy-start(f32[512,1024]{1,0:T(8,128)} %get-tuple-element.254) | copy-start | bytes 6291460
  571.1 4.1 copy-start.5
  573.1 4.1 copy-start.16
  575.1 3.9 copy-start.13
Sparse Core Ops, SparseCore 0:
  176.3 18.7 reduce-scatter.3
  359.8 19.4 reduce-scatter.5
  583.5 20.0 reduce-scatter.7
where the time goes:
time: 686 us; the launch traced here: 678 us
  blocking collectives  405 us (59%)
  matrix products  107 us (16%)
  waiting for transfers between devices  56.3 us (8%)
  between operations  46.8 us (7%)
  local copies, waits for them, and re-layouts  37.3 us (5%)
  other arithmetic  24.4 us (4%)
    psum x3, blocking collectives, first_pass(): single = lax.psum(gram_of(member, work), ('wide', 'narrow'))  120 us
    all_gather x3, blocking collectives, per_device(): lax.all_gather(basis[index], 'wide', axis=2, tiled=True)  92.2 us
    psum x2, blocking collectives, second_pass(): lax.psum((stacked_gram(stacked, work), gram_of(work, work)), ('wide', 'na...  81 us
    reduce_scatter x3, waiting for transfers between devices, per_device(): lax.psum_scatter(partial_rows, 'narrow', scatter_dimension=2, tiled=True)  56.3 us
    psum x1, blocking collectives, per_device(): current_block = lax.psum(gram_of(basis[index], product), ('wide', 'narrow'))  39.6 us
    dot_general x48, matrix products, cholesky_pair(): jnp.dot(lower[row, :], solved, precision=highest, preferred_element_type=...  39.5 us
    psum x1, blocking collectives, per_device(): noise_gram = lax.psum(gram_of(noise, noise), ('wide', 'narrow'))  38.9 us
    dot_general x18, matrix products, contract(): lax.dot_general(left, kernel, (((1,), (1,)), ((), ())), precision=highest...  36.4 us
  transfers between devices with their start and end apart: 3, of which 3 were waited for; matrix products, arithmetic and copies ran while one was open for 0% of the time, Pallas kernels for 0%

commit v1 on v0

v1 whole, which is shorter than its diff:
```python
import functools

import jax
import jax.numpy as jnp
from jax import lax
from jax.experimental import pallas as pl
from jax.experimental.pallas import tpu as pltpu
from jax.sharding import PartitionSpec as P

ITERS = 3
ROOT_STEPS = 30
HI = lax.Precision.HIGHEST
MESH = pl.DeviceIdType.MESH
CACHE_LIMIT = 40 * 2**20
PAIRS = ((0, 0), (1, 1), (2, 2), (0, 1), (0, 2), (1, 2))


def split3(a):
    h = a.astype(jnp.bfloat16)
    r = a - h.astype(jnp.float32)
    m = r.astype(jnp.bfloat16)
    l = (r - m.astype(jnp.float32)).astype(jnp.bfloat16)
    return h, m, l


def precise(a, b, dims):
    x, y = split3(a), split3(b)

    def d(p, q):
        return lax.dot_general(x[p], y[q], (dims, ((), ())), preferred_element_type=jnp.float32)

    return ((d(0, 2) + d(2, 0)) + d(1, 1)) + (d(0, 1) + d(1, 0)) + d(0, 0)


def nn(a, b):
    return precise(a, b, ((1,), (0,)))


def nt(a, b):
    return precise(a, b, ((1,), (1,)))


def nt_low(a, b):
    return lax.dot_general(
        a, b, (((1,), (1,)), ((), ())), preferred_element_type=jnp.float32
    )


def iota(shape, dim):
    return lax.broadcasted_iota(jnp.int32, shape, dim)


def eliminate(k, aug):
    rows = iota(aug.shape, 0)
    lanes = iota(aug.shape, 1)
    pivot_row = jnp.sum(jnp.where(rows == k, aug, 0.0), axis=0, keepdims=True)
    column = jnp.sum(jnp.where(lanes == k, aug, 0.0), axis=1, keepdims=True)
    pivot = jnp.sum(jnp.where(rows[:, :1] == k, column, 0.0), axis=0, keepdims=True)
    scale = lax.rsqrt(pivot)
    scaled = pivot_row * scale
    return jnp.where(
        rows > k, aug - (column * scale) * scaled, jnp.where(rows == k, scaled, aug)
    )


def body(
    wide,
    narrow,
    width,
    cached,
    pos_ref,
    noise_ref,
    out_ref,
    buf,
    rowpos,
    colpos,
    mh,
    ml,
    acc,
    ssem,
    rsem,
):
    count = wide * narrow
    local = pos_ref.shape[1]
    comp = 3 * width
    slab_at = comp
    pos_at = comp + width
    group = 4
    chunks = count // group
    span = group * local
    w = lax.axis_index("wide")
    n = lax.axis_index("narrow")
    me = w * narrow + n
    ny = narrow // 2
    y, core = lax.div(n, 2), lax.rem(n, 2)
    sibling = (w, y * 2 + 1 - core)
    wide_to = [(lax.rem(w + k, wide), n) for k in range(1, wide)]
    y_to = [(w, lax.rem(y + q, ny) * 2 + core) for q in range(1, ny)]

    barrier = pltpu.get_barrier_semaphore()
    peers = wide_to + y_to + [sibling]
    for peer in peers:
        pl.semaphore_signal(barrier, inc=1, device_id=peer, device_id_type=MESH)

    def exchange(par, begin, size):
        sent = []

        def copy(slot, target, index):
            view = buf.at[par, slot, pl.ds(begin, size)]
            return pltpu.make_async_remote_copy(
                src_ref=view,
                dst_ref=view,
                send_sem=ssem.at[par, index],
                recv_sem=rsem.at[par, slot],
                device_id=target,
                device_id_type=MESH,
            )

        def send(slot, target):
            one = copy(slot, target, len(sent))
            one.start()
            sent.append(one)

        def arrived(slot):
            copy(slot, sibling, 0).wait_recv()

        for target in wide_to:
            send(me, target)
        for target in y_to:
            send(me, target)
        send(me, sibling)
        for k in range(1, wide):
            slot = lax.rem(w + wide - k, wide) * narrow + n
            arrived(slot)
            for target in y_to:
                send(slot, target)
            send(slot, sibling)
        for k in range(wide):
            for q in range(1, ny):
                from_y = lax.rem(y + ny - q, ny) * 2 + core
                slot = lax.rem(w + wide - k, wide) * narrow + from_y
                arrived(slot)
                send(slot, sibling)
        for k in range(wide):
            for q in range(ny):
                from_n = lax.rem(y + ny - q, ny) * 2 + 1 - core
                arrived(lax.rem(w + wide - k, wide) * narrow + from_n)
        for one in sent:
            one.wait_send()

    def put_block(par, rows):
        for c in range(3):
            buf[par, me, c * width : (c + 1) * width, :] = rows[:, c * local : (c + 1) * local]

    def put_slab(par, slab):
        pad = jnp.zeros((width, local - slab.shape[1]), jnp.float32)
        buf[par, me, slab_at : slab_at + width, :] = (
            slab if slab.shape[1] == local else jnp.concatenate([slab, pad], axis=1)
        )

    def slab_sum(par):
        def add(d, total):
            return total + buf[par, d, slab_at : slab_at + width, :]

        return lax.fori_loop(0, count, add, jnp.zeros((width, local), jnp.float32))

    def make_tile(chunk, base):
        for t in range(group):
            col = colpos[chunk * group + t]
            for r in range(local // 16):
                rs = slice(r * 16, r * 16 + 16)
                d = [rowpos[c, rs, :] - col[c : c + 1, :] for c in range(3)]
                d2 = d[0] * d[0] + d[1] * d[1] + d[2] * d[2]
                inv = lax.rsqrt(jnp.maximum(d2, 1.0))
                inv2 = inv * inv
                near = d2 < 4.0
                scalar = jnp.where(near, 1.0 - 0.28125 * (d2 * inv), inv * (0.75 + 0.5 * inv2))
                outer = inv * jnp.where(near, 0.09375, (0.75 - 1.5 * inv2) * inv2)
                od = [outer * x for x in d]
                for m, (a, b) in enumerate(PAIRS):
                    value = od[a] * d[b]
                    if a == b:
                        value = value + scalar
                    high = value.astype(jnp.bfloat16)
                    low = (value - high.astype(jnp.float32)).astype(jnp.bfloat16)
                    at = slice(m * local + r * 16, m * local + r * 16 + 16)
                    mh[base, at, t * local : (t + 1) * local] = high
                    ml[base, at, t * local : (t + 1) * local] = low

    def product(par, fresh, aug):
        acc[...] = jnp.zeros_like(acc)
        per = -(-width // chunks)

        def step(chunk, aug):
            base = chunk if cached else 0
            if fresh or not cached:
                make_tile(chunk, base)
            for extra in range(per):
                k = chunk * per + extra
                aug = jnp.where(k < width, eliminate(k, aug), aug)
            v = jnp.concatenate(
                [buf[par, chunk * group + t, 0:comp, :] for t in range(group)], axis=1
            )
            vh = v.astype(jnp.bfloat16)
            vl = (v - vh.astype(jnp.float32)).astype(jnp.bfloat16)
            fill = jnp.zeros((local - 2 * comp, span), jnp.bfloat16)
            both = jnp.concatenate([vh, vl, fill], axis=0)
            acc[...] += nt_low(mh[base], both)
            acc[...] += nt_low(ml[base], both)
            return aug

        aug = lax.fori_loop(0, chunks, step, aug)
        turned = []
        for m in range(6):
            one = jnp.transpose(acc[m * local : (m + 1) * local, :])
            turned.append(one[0:comp] + one[comp : 2 * comp])
        where = {pair: m for m, pair in enumerate(PAIRS)}
        parts = []
        for a in range(3):
            total = None
            for b in range(3):
                m = where[(min(a, b), max(a, b))]
                piece = turned[m][b * width : (b + 1) * width]
                total = piece if total is None else total + piece
            parts.append(total)
        return jnp.concatenate(parts, axis=1), aug

    def hot(shape, shift):
        return jnp.where(iota(shape, 0) + shift == iota(shape, 1), 1.0, 0.0)

    eye = hot((width, width), 0)

    def augmented(gram):
        return jnp.concatenate([gram, eye], axis=1)

    x = jnp.concatenate([noise_ref[c] for c in range(3)], axis=1)
    put_block(0, x)
    put_slab(0, nt(x, x))
    buf[0, me, pos_at : pos_at + 3, :] = pos_ref[...]
    buf[0, me, pos_at + 3 : pos_at + 8, :] = jnp.zeros((5, local), jnp.float32)
    square = jnp.concatenate(
        [pos_ref[...], jnp.zeros((local - 3, local), jnp.float32)], axis=0
    )
    turned_pos = jnp.transpose(square)
    for c in range(3):
        rowpos[c] = jnp.broadcast_to(turned_pos[:, c : c + 1], (local, local))
    acc[...] = jnp.zeros_like(acc)
    pl.semaphore_wait(barrier, len(peers))
    exchange(0, 0, pos_at + 8)

    def keep(d, carry):
        colpos[d] = buf[0, d, pos_at : pos_at + 8, :]
        return carry

    lax.fori_loop(0, count, keep, 0)
    total = slab_sum(0)
    image, aug = product(0, True, augmented(total[:, 0:width]))
    start_upper, linv = aug[:, 0:width], aug[:, width : 2 * width]
    basis = [nn(linv, x)]
    images = [nn(linv, image)]
    diagonal = []
    lower = []
    for j in range(1, ITERS):
        par = j % 2
        work = images[-1]
        lanes = width * (j + 1 + j * j)
        slab = nt(work, jnp.concatenate(basis + [work], axis=0))
        rows = [slab]
        stacked = jnp.concatenate(basis, axis=0)
        for member in basis:
            rows.append(nt(member, stacked))
        placed = jnp.concatenate(rows, axis=1)
        put_block(par, work)
        put_slab(par, placed)
        exchange(par, 0, pos_at)
        total = slab_sum(par)
        ht = total[:, 0 : width * j]
        square_gram = total[:, width * j : width * (j + 1)]
        at = width * (j + 1)
        gram = jnp.concatenate(
            [total[:, at + width * j * m : at + width * j * (m + 1)] for m in range(j)], axis=0
        )
        again = ht - nn(ht, gram)
        ft = ht + again
        diagonal.append(ht[:, width * (j - 1) : width * j])
        left = nt(ft, ht)
        reduced = square_gram - left - nt(ht, ft) + nt(nn(ft, gram), ft)
        image, aug = product(par, False, augmented(reduced))
        upper, linv = aug[:, 0:width], aug[:, width : 2 * width]
        lower.append(upper)
        basis.append(nn(linv, work - nn(ft, stacked)))
        images.append(nn(linv, image - nn(ft, jnp.concatenate(images, axis=0))))
    par = ITERS % 2
    put_slab(par, nt(images[-1], basis[-1]))
    exchange(par, slab_at, width)
    diagonal.append(slab_sum(par)[:, 0:width])

    order = ITERS * width

    strips = []
    for k in range(ITERS):
        cells = [jnp.zeros((width, width), jnp.float32)] * ITERS
        cells[k] = 0.5 * (diagonal[k] + nt(eye, diagonal[k]))
        if k > 0:
            cells[k - 1] = lower[k - 1]
        if k + 1 < ITERS:
            cells[k + 1] = nt(eye, lower[k])
        strips.append(jnp.concatenate(cells, axis=1))
    matrix = jnp.concatenate(strips, axis=0)
    size = jnp.sum(jnp.sum(matrix * matrix, axis=1, keepdims=True), axis=0, keepdims=True)
    scale = jnp.sqrt(size)
    identity = hot((order, order), 0)

    def newton(turn, carry):
        current, other = carry
        factor = 1.5 * identity - 0.5 * nn(other, current)
        return nn(current, factor), nn(factor, other)

    current, other = lax.fori_loop(0, ROOT_STEPS, newton, (matrix / scale, identity))
    mixing = nn(nt(eye, start_upper), current[0:width, :]) * jnp.sqrt(scale)
    result = nn(mixing, jnp.concatenate(basis, axis=0))
    for c in range(3):
        out_ref[c] = result[:, c * local : (c + 1) * local]


def solution(mesh):
    wide, narrow = mesh.shape["wide"], mesh.shape["narrow"]
    count = wide * narrow

    def per_device(positions, noise):
        width, local = noise.shape[1], noise.shape[2]
        comp = 3 * width
        cached = 6 * local * local * count * 4 <= CACHE_LIMIT
        tiles = count // 4 if cached else 1
        return pl.pallas_call(
            functools.partial(body, wide, narrow, width, cached),
            out_shape=jax.ShapeDtypeStruct(noise.shape, jnp.float32),
            in_specs=[pl.BlockSpec(memory_space=pltpu.VMEM)] * 2,
            out_specs=pl.BlockSpec(memory_space=pltpu.VMEM),
            scratch_shapes=[
                pltpu.VMEM((2, count, comp + width + 8, local), jnp.float32),
                pltpu.VMEM((3, local, local), jnp.float32),
                pltpu.VMEM((count, 8, local), jnp.float32),
                pltpu.VMEM((tiles, 6 * local, 4 * local), jnp.bfloat16),
                pltpu.VMEM((tiles, 6 * local, 4 * local), jnp.bfloat16),
                pltpu.VMEM((6 * local, local), jnp.float32),
                pltpu.SemaphoreType.DMA((2, count)),
                pltpu.SemaphoreType.DMA((2, count)),
            ],
            compiler_params=pltpu.CompilerParams(
                collective_id=0, has_side_effects=True, vmem_limit_bytes=60 * 2**20
            ),
        )(positions, noise)

    return jax.shard_map(
        per_device,
        mesh=mesh,
        in_specs=(P(None, ("wide", "narrow")), P(None, None, ("wide", "narrow"))),
        out_specs=P(None, None, ("wide", "narrow")),
        check_vma=False,
    )
```

time: 686 us -> 88.4 us (0.13); the launches traced: 678 us -> 88.1 us
  blocking collectives: 405 us -> 0 us
  matrix products: 107 us -> 0 us
  Pallas kernels: 0 us -> 86.8 us
  waiting for transfers between devices: 56.3 us -> 0 us
  between operations: 46.8 us -> 0.01 us
  local copies, waits for them, and re-layouts: 37.3 us -> 1.35 us
  other arithmetic: 24.4 us -> 0 us
    psum x7 -> x0, blocking collectives: 279 us -> none  [the longest x3 120 us: first_pass(): single = lax.psum(gram_of(member, work), ('wide', 'narrow'))]
    all_gather x5 -> x0, blocking collectives: 126 us -> none  [the longest x3 92.2 us: per_device(): lax.all_gather(basis[index], 'wide', axis=2, tiled=True)]
    dot_general x223 -> x0, matrix products: 107 us -> none  [the longest x48 39.5 us: cholesky_pair(): jnp.dot(lower[row, :], solved, precision=highest, preferred_element_type=...]
    pallas_call x0 -> x1, Pallas kernels: none -> 86.8 us  [per_device(): pl.pallas_call(functools.partial(body, wide, narrow, width, cached), out_...]
    reduce_scatter x3 -> x0, waiting for transfers between devices: 56.3 us -> none  [per_device(): lax.psum_scatter(partial_rows, 'narrow', scatter_dimension=2, tiled=True)]
    slice x51 -> x0, local copies, waits for them, and re-layouts: 30.4 us -> none  [the longest x45 26.8 us: cholesky_pair(): pivot = jnp.sqrt(needed[column])]
    add x57 -> x0, other arithmetic: 12.2 us -> none  [the longest x2 7.32 us: tile_product(): diag_kernel = scalar + outer_part * delta[component] * delta[component]]
  transfers between devices with their start and end apart: 3 -> 0, of which waited for: 3 -> 0; matrix products, arithmetic and copies ran while one was open for 0% -> 0% of each run, Pallas kernels for 0% -> 0%
where the time goes in v1:
time: 88.4 us; the launch traced here: 88.1 us
  Pallas kernels  86.8 us (98%)
  local copies, waits for them, and re-layouts  1.35 us (2%)
    pallas_call x1, Pallas kernels, per_device(): pl.pallas_call(functools.partial(body, wide, narrow, width, cached), out_...  86.8 us

profile of v1, /device:TPU:0, one launch (start us, length us, event | category | flops | bytes accessed | tf_op | source)
XLA Modules:
  0.0 88.1 jit_solution(10854784533459565345)
XLA Ops:
  0.0 86.8 %shard_map.28 = f32[3,16,128]{2,1,0:T(8,128)} custom-call(f32[3,128]{1,0:T(4,128)} %pos_ref.1, f32[3,16,128]{2,1,0:T(8,128)} %noise_ref.1), custom_call_target="tpu_custom_call" | custom-call | tf_op jit(solution)/shard_map/pallas_call | solution.py:335
  86.8 1.3 %copy.4 = f32[3,16,128]{2,1,0:T(8,128)} copy(f32[3,16,128]{2,1,0:T(8,128)} %shard_map.28) | data formatting | bytes 49152

commit v2 on v1

v2 whole, which is shorter than its diff:
```python
import functools

import jax
import jax.numpy as jnp
from jax import lax
from jax.experimental import pallas as pl
from jax.experimental.pallas import tpu as pltpu
from jax.sharding import PartitionSpec as P

ITERS = 3
ROOT_STEPS = 30
HI = lax.Precision.HIGHEST
MESH = pl.DeviceIdType.MESH
CACHE_LIMIT = 50 * 2**20
PAIRS = ((0, 0), (1, 1), (2, 2), (0, 1), (0, 2), (1, 2))


def split3(a):
    h = a.astype(jnp.bfloat16)
    r = a - h.astype(jnp.float32)
    m = r.astype(jnp.bfloat16)
    l = (r - m.astype(jnp.float32)).astype(jnp.bfloat16)
    return h, m, l


def precise(a, b, dims):
    x, y = split3(a), split3(b)

    def d(p, q):
        return lax.dot_general(x[p], y[q], (dims, ((), ())), preferred_element_type=jnp.float32)

    return ((d(0, 2) + d(2, 0)) + d(1, 1)) + (d(0, 1) + d(1, 0)) + d(0, 0)


def nn(a, b):
    return precise(a, b, ((1,), (0,)))


def nt(a, b):
    return precise(a, b, ((1,), (1,)))


def nn_low(a, b):
    return lax.dot_general(
        a, b, (((1,), (0,)), ((), ())), preferred_element_type=jnp.float32
    )


def iota(shape, dim):
    return lax.broadcasted_iota(jnp.int32, shape, dim)


def eliminate(k, aug):
    rows = iota(aug.shape, 0)
    lanes = iota(aug.shape, 1)
    pivot_row = jnp.sum(jnp.where(rows == k, aug, 0.0), axis=0, keepdims=True)
    column = jnp.sum(jnp.where(lanes == k, aug, 0.0), axis=1, keepdims=True)
    pivot = jnp.sum(jnp.where(rows[:, :1] == k, column, 0.0), axis=0, keepdims=True)
    scale = lax.rsqrt(pivot)
    scaled = pivot_row * scale
    return jnp.where(
        rows > k, aug - (column * scale) * scaled, jnp.where(rows == k, scaled, aug)
    )


def body(
    wide,
    narrow,
    width,
    cached,
    pos_ref,
    noise_ref,
    out_ref,
    buf,
    colpos,
    rowpos,
    colcast,
    mh,
    ml,
    vcat,
    stage,
    red,
    sums,
    fin,
    ssem,
    rsem,
):
    local = pos_ref.shape[1]
    comp = 3 * width
    w = lax.axis_index("wide")
    n = lax.axis_index("narrow")
    outer = 4 if wide % 4 == 0 else 1
    inner = wide // outer
    wo, wi = lax.div(w, inner), lax.rem(w, inner)
    outer_at = [lax.rem(wo + k, outer) * inner + wi for k in range(1, outer)]
    inner_at = [wo * inner + lax.rem(wi + k, inner) for k in range(1, inner)]
    wide_at = [lax.rem(w + k, wide) for k in range(1, wide)]
    narrow_at = [lax.rem(n + q, narrow) for q in range(1, narrow)]
    far = (lax.rem(w + 1, wide), n)

    barrier = pltpu.get_barrier_semaphore()
    peers = [(a, n) for a in wide_at] + [(w, b) for b in narrow_at]
    for peer in peers:
        pl.semaphore_signal(barrier, inc=1, device_id=peer, device_id_type=MESH)

    sent = []
    used = [0]
    pos_wide, pos_narrow = 0, wide
    block_at = wide + narrow
    red_at = block_at + ITERS * wide
    sum_at = red_at + ITERS * narrow
    fin_at = sum_at + (ITERS + 1) * narrow

    def make(src, dst, slot, target, index):
        return pltpu.make_async_remote_copy(
            src_ref=src,
            dst_ref=dst,
            send_sem=ssem.at[index],
            recv_sem=rsem.at[slot],
            device_id=target,
            device_id_type=MESH,
        )

    def send(src, dst, slot, target):
        one = make(src, dst, slot, target, used[0])
        used[0] += 1
        one.start()
        sent.append(one)

    def arrived(dst, slot):
        make(dst, dst, slot, far, 0).wait_recv()

    def put_block(e, rows):
        for c in range(3):
            buf[e, w, c * width : (c + 1) * width, :] = rows[:, c * local : (c + 1) * local]

    def padded(slab):
        if slab.shape[1] == local:
            return slab
        pad = jnp.zeros((width, local - slab.shape[1]), jnp.float32)
        return jnp.concatenate([slab, pad], axis=1)

    def gather(e, direct):
        mine = buf.at[e, w]
        for a in wide_at if direct else outer_at + inner_at:
            send(mine, mine, block_at + e * wide + w, (a, n))

    def gathered(e, direct):
        base = block_at + e * wide
        if direct:
            for k in range(1, wide):
                a = lax.rem(w + wide - k, wide)
                arrived(buf.at[e, a], base + a)
            return
        for a in outer_at:
            view = buf.at[e, a]
            arrived(view, base + a)
            for b in inner_at:
                send(view, view, base + a, (b, n))
        for o in range(outer):
            for k in range(1, inner):
                a = lax.rem(wo + o, outer) * inner + lax.rem(wi + k, inner)
                arrived(buf.at[e, a], base + a)

    def spread_sum(e, total):
        sums[e, n] = total
        view = sums.at[e, n]
        for b in narrow_at:
            send(view, view, sum_at + e * narrow + n, (w, b))

    def narrow_sum(e):
        for b in narrow_at:
            arrived(sums.at[e, b], sum_at + e * narrow + b)
        total = sums[e, 0]
        for b in range(1, narrow):
            total = total + sums[e, b]
        return total

    def make_tile(blocks):
        def one(slot, carry):
            square = jnp.concatenate(
                [colpos[slot], jnp.zeros((local - 8, local), jnp.float32)], axis=0
            )
            turned = jnp.transpose(square)
            for c in range(3):
                colcast[c] = jnp.broadcast_to(turned[:, c : c + 1], (local, local))
            for nb, base in blocks:
                row = rowpos[nb]
                for r in range(local // 16):
                    rs = slice(r * 16, r * 16 + 16)
                    d = [row[c : c + 1, :] - colcast[c, rs, :] for c in range(3)]
                    d2 = d[0] * d[0] + d[1] * d[1] + d[2] * d[2]
                    inv = lax.rsqrt(jnp.maximum(d2, 1.0))
                    inv2 = inv * inv
                    near = d2 < 4.0
                    scalar = jnp.where(
                        near, 1.0 - 0.28125 * (d2 * inv), inv * (0.75 + 0.5 * inv2)
                    )
                    part = inv * jnp.where(near, 0.09375, (0.75 - 1.5 * inv2) * inv2)
                    od = [part * x for x in d]
                    at = pl.ds(pl.multiple_of(slot * local + r * 16, 16), 16)
                    for m, (a, b) in enumerate(PAIRS):
                        value = od[a] * d[b]
                        if a == b:
                            value = value + scalar
                        high = value.astype(jnp.bfloat16)
                        low = (value - high.astype(jnp.float32)).astype(jnp.bfloat16)
                        mh[base, at, m * local : (m + 1) * local] = high
                        ml[base, at, m * local : (m + 1) * local] = low
            return carry

        lax.fori_loop(0, wide, one, 0)

    where = {pair: m for m, pair in enumerate(PAIRS)}

    def product(e, solve):
        for slot in range(wide):
            v = buf[e, slot, 0:comp, :]
            vh = v.astype(jnp.bfloat16)
            vcat[0:comp, slot * local : (slot + 1) * local] = vh
            vcat[comp : 2 * comp, slot * local : (slot + 1) * local] = (
                v - vh.astype(jnp.float32)
            ).astype(jnp.bfloat16)
        aug = None
        step = 0
        own = None
        for q in range(1, narrow + 1):
            nb = lax.rem(n + q, narrow)
            if not cached:
                make_tile([(nb, 0)])
            base = nb if cached else 0
            both = nn_low(vcat[...], mh[base])
            result = both[0:comp] + both[comp : 2 * comp] + nn_low(vcat[0:comp, :], ml[base])
            parts = []
            for a in range(3):
                total = None
                for b in range(3):
                    m = where[(min(a, b), max(a, b))]
                    piece = result[b * width : (b + 1) * width, m * local : (m + 1) * local]
                    total = piece if total is None else total + piece
                parts.append(total)
            if q < narrow:
                for a in range(3):
                    stage[e, q, a * width : (a + 1) * width, :] = parts[a]
                send(stage.at[e, q], red.at[e, n], red_at + e * narrow + n, (w, nb))
            else:
                own = parts
            if q == 1:
                aug = solve()
            else:
                upto = -(-width * (q - 1) // (narrow - 1))
                while step < min(upto, width):
                    aug = eliminate(step, aug)
                    step += 1
        for b in narrow_at:
            arrived(red.at[e, b], red_at + e * narrow + b)
            own = [own[a] + red[e, b, a * width : (a + 1) * width, :] for a in range(3)]
        return jnp.concatenate(own, axis=1), aug

    def hot(shape, shift):
        return jnp.where(iota(shape, 0) + shift == iota(shape, 1), 1.0, 0.0)

    eye = hot((width, width), 0)

    def augmented(gram):
        return jnp.concatenate([gram, eye], axis=1)

    def slab_sum(e):
        total = buf[e, 0, comp : comp + width, :]
        for a in range(1, wide):
            total = total + buf[e, a, comp : comp + width, :]
        return total

    places = jnp.concatenate([pos_ref[...], jnp.zeros((5, local), jnp.float32)], axis=0)
    colpos[w] = places
    rowpos[n] = places
    x = jnp.concatenate([noise_ref[c] for c in range(3)], axis=1)
    put_block(0, x)
    buf[0, w, comp : comp + width, :] = padded(nt(x, x))
    pl.semaphore_wait(barrier, len(peers))
    for a in wide_at:
        send(colpos.at[w], colpos.at[w], pos_wide + w, (a, n))
    for b in narrow_at:
        send(rowpos.at[n], rowpos.at[n], pos_narrow + n, (w, b))
    gather(0, True)
    for b in narrow_at:
        arrived(rowpos.at[b], pos_narrow + b)
    for a in wide_at:
        arrived(colpos.at[a], pos_wide + a)
    if cached:
        make_tile([(nb, nb) for nb in range(narrow)])
    gathered(0, True)
    spread_sum(0, slab_sum(0))
    image, aug = product(0, lambda: augmented(narrow_sum(0)[:, 0:width]))
    start_upper, linv = aug[:, 0:width], aug[:, width : 2 * width]
    basis = [nn(linv, x)]
    images = [nn(linv, image)]
    diagonal = []
    lower = []
    for j in range(1, ITERS):
        work = images[-1]
        stacked = jnp.concatenate(basis, axis=0)
        put_block(j, work)
        rows = [nt(work, jnp.concatenate(basis + [work], axis=0))]
        for member in basis:
            rows.append(nt(member, stacked))
        buf[j, w, comp : comp + width, :] = padded(jnp.concatenate(rows, axis=1))
        gather(j, False)
        gathered(j, False)
        spread_sum(j, slab_sum(j))
        kept = {}

        def solve():
            total = narrow_sum(j)
            ht = total[:, 0 : width * j]
            square_gram = total[:, width * j : width * (j + 1)]
            at = width * (j + 1)
            gram = jnp.concatenate(
                [total[:, at + width * j * m : at + width * j * (m + 1)] for m in range(j)],
                axis=0,
            )
            again = ht - nn(ht, gram)
            ft = ht + again
            kept["ft"] = ft
            diagonal.append(ht[:, width * (j - 1) : width * j])
            reduced = square_gram - nt(ft, ht) - nt(ht, ft) + nt(nn(ft, gram), ft)
            return augmented(reduced)

        image, aug = product(j, solve)
        ft = kept["ft"]
        upper, linv = aug[:, 0:width], aug[:, width : 2 * width]
        lower.append(upper)
        basis.append(nn(linv, work - nn(ft, stacked)))
        images.append(nn(linv, image - nn(ft, jnp.concatenate(images, axis=0))))
    fin[w] = padded(nt(images[-1], basis[-1]))
    for a in wide_at:
        send(fin.at[w], fin.at[w], fin_at + w, (a, n))
    for a in wide_at:
        arrived(fin.at[a], fin_at + a)
    total = fin[0]
    for a in range(1, wide):
        total = total + fin[a]
    spread_sum(ITERS, total)
    diagonal.append(narrow_sum(ITERS)[:, 0:width])

    order = ITERS * width

    strips = []
    for k in range(ITERS):
        cells = [jnp.zeros((width, width), jnp.float32)] * ITERS
        cells[k] = 0.5 * (diagonal[k] + nt(eye, diagonal[k]))
        if k > 0:
            cells[k - 1] = lower[k - 1]
        if k + 1 < ITERS:
            cells[k + 1] = nt(eye, lower[k])
        strips.append(jnp.concatenate(cells, axis=1))
    matrix = jnp.concatenate(strips, axis=0)
    size = jnp.sum(jnp.sum(matrix * matrix, axis=1, keepdims=True), axis=0, keepdims=True)
    scale = jnp.sqrt(size)
    identity = hot((order, order), 0)

    def newton(turn, carry):
        current, other = carry
        factor = 1.5 * identity - 0.5 * nn(other, current)
        return nn(current, factor), nn(factor, other)

    current, other = lax.fori_loop(0, ROOT_STEPS, newton, (matrix / scale, identity))
    mixing = nn(nt(eye, start_upper), current[0:width, :]) * jnp.sqrt(scale)
    result = nn(mixing, jnp.concatenate(basis, axis=0))
    for c in range(3):
        out_ref[c] = result[:, c * local : (c + 1) * local]
    for one in sent:
        one.wait_send()


def solution(mesh):
    wide, narrow = mesh.shape["wide"], mesh.shape["narrow"]
    count = wide * narrow

    def per_device(positions, noise):
        width, local = noise.shape[1], noise.shape[2]
        comp = 3 * width
        cached = 6 * local * local * count * 4 <= CACHE_LIMIT
        tiles = narrow if cached else 1
        received = wide + narrow + ITERS * (wide + narrow) + (ITERS + 1) * narrow + wide
        f32 = jnp.float32
        return pl.pallas_call(
            functools.partial(body, wide, narrow, width, cached),
            out_shape=jax.ShapeDtypeStruct(noise.shape, f32),
            in_specs=[pl.BlockSpec(memory_space=pltpu.VMEM)] * 2,
            out_specs=pl.BlockSpec(memory_space=pltpu.VMEM),
            scratch_shapes=[
                pltpu.VMEM((ITERS, wide, comp + width, local), f32),
                pltpu.VMEM((wide, 8, local), f32),
                pltpu.VMEM((narrow, 8, local), f32),
                pltpu.VMEM((3, local, local), f32),
                pltpu.VMEM((tiles, wide * local, 6 * local), jnp.bfloat16),
                pltpu.VMEM((tiles, wide * local, 6 * local), jnp.bfloat16),
                pltpu.VMEM((2 * comp, wide * local), jnp.bfloat16),
                pltpu.VMEM((ITERS, narrow, comp, local), f32),
                pltpu.VMEM((ITERS, narrow, comp, local), f32),
                pltpu.VMEM((ITERS + 1, narrow, width, local), f32),
                pltpu.VMEM((wide, width, local), f32),
                pltpu.SemaphoreType.DMA((2 * received,)),
                pltpu.SemaphoreType.DMA((received,)),
            ],
            compiler_params=pltpu.CompilerParams(
                collective_id=0, has_side_effects=True, vmem_limit_bytes=60 * 2**20
            ),
        )(positions, noise)

    return jax.shard_map(
        per_device,
        mesh=mesh,
        in_specs=(P(None, ("wide", "narrow")), P(None, None, ("wide", "narrow"))),
        out_specs=P(None, None, ("wide", "narrow")),
        check_vma=False,
    )
```

time: 88.4 us -> 80 us (0.905)
  Pallas kernels: 86.8 us -> 78.4 us
    pallas_call x1, Pallas kernels: 86.8 us -> 78.4 us  [per_device(): pl.pallas_call(functools.partial(body, wide, narrow, width, cached), out_...]
where the time goes in v2:
time: 80 us; the launch traced here: 79.8 us
  Pallas kernels  78.4 us (98%)
  local copies, waits for them, and re-layouts  1.35 us (2%)
    pallas_call x1, Pallas kernels, per_device(): pl.pallas_call(functools.partial(body, wide, narrow, width, cached), out_...  78.4 us

profile of v2, /device:TPU:0, one launch (start us, length us, event | category | flops | bytes accessed | tf_op | source)
XLA Modules:
  0.0 79.8 jit_solution(2336866063044571661)
XLA Ops:
  0.0 78.4 %shard_map.28 = f32[3,16,128]{2,1,0:T(8,128)} custom-call(f32[3,128]{1,0:T(4,128)} %pos_ref.1, f32[3,16,128]{2,1,0:T(8,128)} %noise_ref.1), custom_call_target="tpu_custom_call" | custom-call | tf_op jit(solution)/shard_map/pallas_call | solution.py:387
  78.5 1.3 %copy.4 = f32[3,16,128]{2,1,0:T(8,128)} copy(f32[3,16,128]{2,1,0:T(8,128)} %shard_map.28) | data formatting | bytes 49152

commit v3 on v2

--- a/solution.py
+++ b/solution.py
@@ -23,21 +23,27 @@
     return h, m, l
 
 
-def precise(a, b, dims):
-    x, y = split3(a), split3(b)
+def precise(a, parts, dims):
+    rows = a.shape[0]
+    left = split3(a)
+    yh, ym, yl = parts
 
     def d(p, q):
-        return lax.dot_general(x[p], y[q], (dims, ((), ())), preferred_element_type=jnp.float32)
-
-    return ((d(0, 2) + d(2, 0)) + d(1, 1)) + (d(0, 1) + d(1, 0)) + d(0, 0)
+        return lax.dot_general(p, q, (dims, ((), ())), preferred_element_type=jnp.float32)
+
+    first = d(jnp.concatenate(left, axis=0), yh)
+    second = d(jnp.concatenate(left[:2], axis=0), ym)
+    third = d(left[0], yl)
+    small = (third + first[2 * rows :]) + second[rows:]
+    return (small + (second[:rows] + first[rows : 2 * rows])) + first[:rows]
 
 
 def nn(a, b):
-    return precise(a, b, ((1,), (0,)))
+    return precise(a, split3(b), ((1,), (0,)))
 
 
 def nt(a, b):
-    return precise(a, b, ((1,), (1,)))
+    return precise(a, split3(b), ((1,), (1,)))
 
 
 def nn_low(a, b):
@@ -89,11 +95,6 @@
     comp = 3 * width
     w = lax.axis_index("wide")
     n = lax.axis_index("narrow")
-    outer = 4 if wide % 4 == 0 else 1
-    inner = wide // outer
-    wo, wi = lax.div(w, inner), lax.rem(w, inner)
-    outer_at = [lax.rem(wo + k, outer) * inner + wi for k in range(1, outer)]
-    inner_at = [wo * inner + lax.rem(wi + k, inner) for k in range(1, inner)]
     wide_at = [lax.rem(w + k, wide) for k in range(1, wide)]
     narrow_at = [lax.rem(n + q, narrow) for q in range(1, narrow)]
     far = (lax.rem(w + 1, wide), n)
@@ -140,43 +141,41 @@
         pad = jnp.zeros((width, local - slab.shape[1]), jnp.float32)
         return jnp.concatenate([slab, pad], axis=1)
 
-    def gather(e, direct):
+    def gather(e):
         mine = buf.at[e, w]
-        for a in wide_at if direct else outer_at + inner_at:
+        for a in wide_at:
             send(mine, mine, block_at + e * wide + w, (a, n))
 
-    def gathered(e, direct):
-        base = block_at + e * wide
-        if direct:
-            for k in range(1, wide):
-                a = lax.rem(w + wide - k, wide)
-                arrived(buf.at[e, a], base + a)
-            return
-        for a in outer_at:
-            view = buf.at[e, a]
-            arrived(view, base + a)
-            for b in inner_at:
-                send(view, view, base + a, (b, n))
-        for o in range(outer):
-            for k in range(1, inner):
-                a = lax.rem(wo + o, outer) * inner + lax.rem(wi + k, inner)
-                arrived(buf.at[e, a], base + a)
-
-    def spread_sum(e, total):
-        sums[e, n] = total
+    def gathered(e):
+        for a in reversed(wide_at):
+            arrived(buf.at[e, a], block_at + e * wide + a)
+
+    def add_narrow(e, slab):
+        sums[e, n] = padded(slab)
         view = sums.at[e, n]
         for b in narrow_at:
             send(view, view, sum_at + e * narrow + n, (w, b))
 
-    def narrow_sum(e):
+    def add_wide(e):
         for b in narrow_at:
             arrived(sums.at[e, b], sum_at + e * narrow + b)
         total = sums[e, 0]
         for b in range(1, narrow):
             total = total + sums[e, b]
+        fin[e, w] = total
+        view = fin.at[e, w]
+        for a in wide_at:
+            send(view, view, fin_at + e * wide + w, (a, n))
+
+    def added(e):
+        for a in reversed(wide_at):
+            arrived(fin.at[e, a], fin_at + e * wide + a)
+        total = fin[e, 0]
+        for a in range(1, wide):
+            total = total + fin[e, a]
         return total
 
-    def make_tile(blocks):
+    def make_tile(single):
         def one(slot, carry):
             square = jnp.concatenate(
                 [colpos[slot], jnp.zeros((local - 8, local), jnp.float32)], axis=0
@@ -184,7 +183,9 @@
             turned = jnp.transpose(square)
             for c in range(3):
                 colcast[c] = jnp.broadcast_to(turned[:, c : c + 1], (local, local))
-            for nb, base in blocks:
+            def block(index, inner_carry):
+                nb = index if cached else single
+                base = index if cached else 0
                 row = rowpos[nb]
                 for r in range(local // 16):
                     rs = slice(r * 16, r * 16 + 16)
@@ -207,6 +208,9 @@
                         low = (value - high.astype(jnp.float32)).astype(jnp.bfloat16)
                         mh[base, at, m * local : (m + 1) * local] = high
                         ml[base, at, m * local : (m + 1) * local] = low
+                return inner_carry
+
+            lax.fori_loop(0, narrow if cached else 1, block, 0)
             return carry
 
         lax.fori_loop(0, wide, one, 0)
@@ -227,7 +231,7 @@
         for q in range(1, narrow + 1):
             nb = lax.rem(n + q, narrow)
             if not cached:
-                make_tile([(nb, 0)])
+                make_tile(nb)
             base = nb if cached else 0
             both = nn_low(vcat[...], mh[base])
             result = both[0:comp] + both[comp : 2 * comp] + nn_low(vcat[0:comp, :], ml[base])
@@ -265,33 +269,27 @@
     def augmented(gram):
         return jnp.concatenate([gram, eye], axis=1)
 
-    def slab_sum(e):
-        total = buf[e, 0, comp : comp + width, :]
-        for a in range(1, wide):
-            total = total + buf[e, a, comp : comp + width, :]
-        return total
-
     places = jnp.concatenate([pos_ref[...], jnp.zeros((5, local), jnp.float32)], axis=0)
     colpos[w] = places
     rowpos[n] = places
     x = jnp.concatenate([noise_ref[c] for c in range(3)], axis=1)
     put_block(0, x)
-    buf[0, w, comp : comp + width, :] = padded(nt(x, x))
     pl.semaphore_wait(barrier, len(peers))
     for a in wide_at:
         send(colpos.at[w], colpos.at[w], pos_wide + w, (a, n))
     for b in narrow_at:
         send(rowpos.at[n], rowpos.at[n], pos_narrow + n, (w, b))
-    gather(0, True)
+    gather(0)
+    add_narrow(0, nt(x, x))
     for b in narrow_at:
         arrived(rowpos.at[b], pos_narrow + b)
+    add_wide(0)
     for a in wide_at:
         arrived(colpos.at[a], pos_wide + a)
     if cached:
-        make_tile([(nb, nb) for nb in range(narrow)])
-    gathered(0, True)
-    spread_sum(0, slab_sum(0))
-    image, aug = product(0, lambda: augmented(narrow_sum(0)[:, 0:width]))
+        make_tile(None)
+    gathered(0)
+    image, aug = product(0, lambda: augmented(added(0)[:, 0:width]))
     start_upper, linv = aug[:, 0:width], aug[:, width : 2 * width]
     basis = [nn(linv, x)]
     images = [nn(linv, image)]
@@ -301,17 +299,17 @@
         work = images[-1]
         stacked = jnp.concatenate(basis, axis=0)
         put_block(j, work)
+        gather(j)
         rows = [nt(work, jnp.concatenate(basis + [work], axis=0))]
         for member in basis:
             rows.append(nt(member, stacked))
-        buf[j, w, comp : comp + width, :] = padded(jnp.concatenate(rows, axis=1))
-        gather(j, False)
-        gathered(j, False)
-        spread_sum(j, slab_sum(j))
+        add_narrow(j, jnp.concatenate(rows, axis=1))
+        add_wide(j)
+        gathered(j)
         kept = {}
 
         def solve():
-            total = narrow_sum(j)
+            total = added(j)
             ht = total[:, 0 : width * j]
             square_gram = total[:, width * j : width * (j + 1)]
             at = width * (j + 1)
@@ -332,16 +330,9 @@
         lower.append(upper)
         basis.append(nn(linv, work - nn(ft, stacked)))
         images.append(nn(linv, image - nn(ft, jnp.concatenate(images, axis=0))))
-    fin[w] = padded(nt(images[-1], basis[-1]))
-    for a in wide_at:
-        send(fin.at[w], fin.at[w], fin_at + w, (a, n))
-    for a in wide_at:
-        arrived(fin.at[a], fin_at + a)
-    total = fin[0]
-    for a in range(1, wide):
-        total = total + fin[a]
-    spread_sum(ITERS, total)
-    diagonal.append(narrow_sum(ITERS)[:, 0:width])
+    add_narrow(ITERS, nt(images[-1], basis[-1]))
+    add_wide(ITERS)
+    diagonal.append(added(ITERS)[:, 0:width])
 
     order = ITERS * width
 
@@ -360,12 +351,14 @@
     identity = hot((order, order), 0)
 
     def newton(turn, carry):
-        current, other = carry
-        factor = 1.5 * identity - 0.5 * nn(other, current)
-        return nn(current, factor), nn(factor, other)
-
-    current, other = lax.fori_loop(0, ROOT_STEPS, newton, (matrix / scale, identity))
-    mixing = nn(nt(eye, start_upper), current[0:width, :]) * jnp.sqrt(scale)
+        both, top = carry
+        factor = split3(1.5 * identity - 0.5 * both)
+        turned = precise(jnp.concatenate([both, top], axis=0), factor, ((1,), (0,)))
+        return precise(turned[0:order], factor, ((1,), (0,))), turned[order:]
+
+    start = matrix / scale
+    both, top = lax.fori_loop(0, ROOT_STEPS, newton, (start, start[0:width, :]))
+    mixing = nn(nt(eye, start_upper), top) * jnp.sqrt(scale)
     result = nn(mixing, jnp.concatenate(basis, axis=0))
     for c in range(3):
         out_ref[c] = result[:, c * local : (c + 1) * local]
@@ -382,7 +375,7 @@
         comp = 3 * width
         cached = 6 * local * local * count * 4 <= CACHE_LIMIT
         tiles = narrow if cached else 1
-        received = wide + narrow + ITERS * (wide + narrow) + (ITERS + 1) * narrow + wide
+        received = (2 * ITERS + 2) * (wide + narrow)
         f32 = jnp.float32
         return pl.pallas_call(
             functools.partial(body, wide, narrow, width, cached),
@@ -390,7 +383,7 @@
             in_specs=[pl.BlockSpec(memory_space=pltpu.VMEM)] * 2,
             out_specs=pl.BlockSpec(memory_space=pltpu.VMEM),
             scratch_shapes=[
-                pltpu.VMEM((ITERS, wide, comp + width, local), f32),
+                pltpu.VMEM((ITERS, wide, comp, local), f32),
                 pltpu.VMEM((wide, 8, local), f32),
                 pltpu.VMEM((narrow, 8, local), f32),
                 pltpu.VMEM((3, local, local), f32),
@@ -400,8 +393,8 @@
                 pltpu.VMEM((ITERS, narrow, comp, local), f32),
                 pltpu.VMEM((ITERS, narrow, comp, local), f32),
                 pltpu.VMEM((ITERS + 1, narrow, width, local), f32),
-                pltpu.VMEM((wide, width, local), f32),
-                pltpu.SemaphoreType.DMA((2 * received,)),
+                pltpu.VMEM((ITERS + 1, wide, width, local), f32),
+                pltpu.SemaphoreType.DMA((received,)),
                 pltpu.SemaphoreType.DMA((received,)),
             ],
             compiler_params=pltpu.CompilerParams(

time: 80 us -> 71.2 us (0.89)
  Pallas kernels: 78.4 us -> 69.6 us
    pallas_call x1, Pallas kernels: 78.4 us -> 69.6 us  [per_device(): pl.pallas_call(functools.partial(body, wide, narrow, width, cached), out_...]
where the time goes in v3:
time: 71.2 us; the launch traced here: 71 us
  Pallas kernels  69.6 us (98%)
  local copies, waits for them, and re-layouts  1.35 us (2%)
    pallas_call x1, Pallas kernels, per_device(): pl.pallas_call(functools.partial(body, wide, narrow, width, cached), out_...  69.6 us

profile of v3, /device:TPU:0, one launch (start us, length us, event | category | flops | bytes accessed | tf_op | source)
XLA Modules:
  0.0 71.0 jit_solution(6781242284063265969)
XLA Ops:
  0.0 69.6 %shard_map.28 = f32[3,16,128]{2,1,0:T(8,128)} custom-call(f32[3,128]{1,0:T(4,128)} %pos_ref.1, f32[3,16,128]{2,1,0:T(8,128)} %noise_ref.1), custom_call_target="tpu_custom_call" | custom-call | tf_op jit(solution)/shard_map/pallas_call | solution.py:380
  69.6 1.3 %copy.4 = f32[3,16,128]{2,1,0:T(8,128)} copy(f32[3,16,128]{2,1,0:T(8,128)} %shard_map.28) | data formatting | bytes 49152
